TPU v7x, 16 devices: a whole 2x2x2 slice. The times are simulated.
16 devices in a mesh: row: 2 (over z), col: 8 (over y, x, core).
Axes of the slice: x: 2, y: 2, z: 2, core: 2. Of those that a mesh axis runs over, the one named last changes fastest.
Arguments:
- v_mat: float32 [8192, 8192], P('row', 'col')
- t_fac: float32 [64, 128, 128], P('col')
- z_vec: float32 [8192, 2048], P(None, ('col', 'row'))
Outputs:
- output: float32 [8192, 2048], P('row', 'col')
All inputs are finite; a program needn't handle non-finite values.
Results may differ from a plain program's by a relative error of at most 0.001.
Values sent between devices are 32-bit elements.
A program may use at most 1 GiB of HBM per device.

v0:
```python
import jax
import jax.numpy as jnp
from jax import lax
from jax.sharding import PartitionSpec as P

FULL_PREC = lax.Precision.HIGHEST


def solution(mesh):
    col_shards = mesh.shape['col']

    def local_body(v_loc, t_loc, z_loc):
        panel_width = t_loc.shape[1]
        local_panels = t_loc.shape[0]
        num_panels = local_panels * col_shards
        my_col = lax.axis_index('col')
        t_all = lax.all_gather(t_loc, 'col', axis=0, tiled=True)
        x_loc = lax.all_to_all(z_loc, 'row', 0, 1, tiled=True)

        def panel_step(step_idx, x_cur):
            panel_idx = num_panels - 1 - step_idx
            owner_col = panel_idx % col_shards
            loc_slot = panel_idx // col_shards
            v_blk = lax.dynamic_slice_in_dim(v_loc, loc_slot * panel_width, panel_width, axis=1)
            v_pan = lax.psum(jnp.where(my_col == owner_col, v_blk, 0.0), 'col')
            t_pan = lax.dynamic_index_in_dim(t_all, owner_col * local_panels + loc_slot, axis=0, keepdims=False)
            w_part = jnp.einsum('nb,nk->bk', v_pan, x_cur, preferred_element_type=jnp.float32, precision=FULL_PREC)
            w_full = lax.psum(w_part, 'row')
            y_blk = jnp.dot(t_pan, w_full, preferred_element_type=jnp.float32, precision=FULL_PREC)
            return x_cur - jnp.dot(v_pan, y_blk, preferred_element_type=jnp.float32, precision=FULL_PREC)

        return lax.fori_loop(0, num_panels, panel_step, x_loc)

    return jax.shard_map(local_body, mesh=mesh,
                         in_specs=(P('row', 'col'), P('col', None, None), P(None, ('col', 'row'))),
                         out_specs=P('row', 'col'), check_vma=False)
```

profile of v0, /device:TPU:5, one launch (start us, length us, event | category | flops | bytes accessed | tf_op | source)
XLA Modules:
  0.0 5804.1 jit_solution(11575943312132722055)
XLA Ops:
  70.7 5726.9 %while.15 = (s32[]{:T(128)}, f32[4096,256]{1,0:T(8,128)}, s32[]{:T(128)}, f32[4096,1024]{1,0:T(8,128)}, f32[64,128,128]{2,1,0:T(8,128)}, /*index=5*/s32[]{:T(128...) while((s32[]{:T(128)}, f32[4096,256]{1,0:T(8,128)}, ...), condition=%wide.region_3.4_spmd, body=%wide.region_0.3_spmd.sunk | while | flops 3273687040 | bytes 43319864 | solution.py:32
  73.9 53.5 all-reduce.3.cloned.1.call-done
  342.4 53.2 all-reduce.3.cloned.1.call-done
  968.0 53.2 all-reduce.3.cloned.1.call-done
  1236.3 53.2 all-reduce.3.cloned.1.call-done
  1415.2 53.2 all-reduce.3.cloned.1.call-done
  1504.8 53.2 all-reduce.3.cloned.1.call-done
  1683.8 53.2 all-reduce.3.cloned.1.call-done
  1773.4 53.2 all-reduce.3.cloned.1.call-done
  1863.1 53.2 all-reduce.3.cloned.1.call-done
  1952.7 53.2 all-reduce.3.cloned.1.call-done
  2220.9 53.2 all-reduce.3.cloned.1.call-done
  2489.8 53.2 all-reduce.3.cloned.1.call-done
  2668.8 53.2 all-reduce.3.cloned.1.call-done
  2758.4 53.2 all-reduce.3.cloned.1.call-done
  3026.6 53.2 all-reduce.3.cloned.1.call-done
  3473.5 53.2 all-reduce.3.cloned.1.call-done
  3563.1 53.2 all-reduce.3.cloned.1.call-done
  4010.0 53.2 all-reduce.3.cloned.1.call-done
  4189.0 53.2 all-reduce.3.cloned.1.call-done
  4278.6 53.2 all-reduce.3.cloned.1.call-done
  4546.9 53.2 all-reduce.3.cloned.1.call-done
  4725.8 53.2 all-reduce.3.cloned.1.call-done
  4815.5 53.2 all-reduce.3.cloned.1.call-done
  4905.1 53.2 all-reduce.3.cloned.1.call-done
  4994.7 53.2 all-reduce.3.cloned.1.call-done
  5084.3 53.2 all-reduce.3.cloned.1.call-done
  5174.0 53.2 all-reduce.3.cloned.1.call-done
  5352.9 53.2 all-reduce.3.cloned.1.call-done
  5442.5 53.2 all-reduce.3.cloned.1.call-done
  5621.5 53.2 all-reduce.3.cloned.1.call-done
  5711.1 53.2 all-reduce.3.cloned.1.call-done
  (744 shorter events, 4138.8 us)
Async XLA Ops:
  73.8 79.1 %all-reduce.5.cloned.1.call-start = ((), (), s32[]{:S(2)}) async-start(), calls=%async_computation.3 | async-start | bytes 262144 | tf_op jit(solution)/shard_map/while/body/eval_jaxpr/psum | solution.py:28
  342.4 78.8 %all-reduce.5.cloned.1.call-start = ((), (), s32[]{:S(2)}) async-start(), calls=%async_computation.3 | async-start | bytes 262144 | tf_op jit(solution)/shard_map/while/body/eval_jaxpr/psum | solution.py:28
  967.9 78.8 %all-reduce.5.cloned.1.call-start = ((), (), s32[]{:S(2)}) async-start(), calls=%async_computation.3 | async-start | bytes 262144 | tf_op jit(solution)/shard_map/while/body/eval_jaxpr/psum | solution.py:28
  1236.2 78.8 %all-reduce.5.cloned.1.call-start = ((), (), s32[]{:S(2)}) async-start(), calls=%async_computation.3 | async-start | bytes 262144 | tf_op jit(solution)/shard_map/while/body/eval_jaxpr/psum | solution.py:28
  1415.2 78.8 %all-reduce.5.cloned.1.call-start = ((), (), s32[]{:S(2)}) async-start(), calls=%async_computation.3 | async-start | bytes 262144 | tf_op jit(solution)/shard_map/while/body/eval_jaxpr/psum | solution.py:28
  1504.8 78.8 %all-reduce.5.cloned.1.call-start = ((), (), s32[]{:S(2)}) async-start(), calls=%async_computation.3 | async-start | bytes 262144 | tf_op jit(solution)/shard_map/while/body/eval_jaxpr/psum | solution.py:28
  1683.7 78.8 %all-reduce.5.cloned.1.call-start = ((), (), s32[]{:S(2)}) async-start(), calls=%async_computation.3 | async-start | bytes 262144 | tf_op jit(solution)/shard_map/while/body/eval_jaxpr/psum | solution.py:28
  1773.4 78.8 %all-reduce.5.cloned.1.call-start = ((), (), s32[]{:S(2)}) async-start(), calls=%async_computation.3 | async-start | bytes 262144 | tf_op jit(solution)/shard_map/while/body/eval_jaxpr/psum | solution.py:28
  1863.0 78.8 %all-reduce.5.cloned.1.call-start = ((), (), s32[]{:S(2)}) async-start(), calls=%async_computation.3 | async-start | bytes 262144 | tf_op jit(solution)/shard_map/while/body/eval_jaxpr/psum | solution.py:28
  1952.6 78.8 %all-reduce.5.cloned.1.call-start = ((), (), s32[]{:S(2)}) async-start(), calls=%async_computation.3 | async-start | bytes 262144 | tf_op jit(solution)/shard_map/while/body/eval_jaxpr/psum | solution.py:28
  2220.9 78.8 %all-reduce.5.cloned.1.call-start = ((), (), s32[]{:S(2)}) async-start(), calls=%async_computation.3 | async-start | bytes 262144 | tf_op jit(solution)/shard_map/while/body/eval_jaxpr/psum | solution.py:28
  2400.1 78.8 %all-reduce.5.cloned.1.call-start = ((), (), s32[]{:S(2)}) async-start(), calls=%async_computation.3 | async-start | bytes 262144 | tf_op jit(solution)/shard_map/while/body/eval_jaxpr/psum | solution.py:28
  2489.7 78.8 %all-reduce.5.cloned.1.call-start = ((), (), s32[]{:S(2)}) async-start(), calls=%async_computation.3 | async-start | bytes 262144 | tf_op jit(solution)/shard_map/while/body/eval_jaxpr/psum | solution.py:28
  2668.7 78.8 %all-reduce.5.cloned.1.call-start = ((), (), s32[]{:S(2)}) async-start(), calls=%async_computation.3 | async-start | bytes 262144 | tf_op jit(solution)/shard_map/while/body/eval_jaxpr/psum | solution.py:28
  2758.3 78.8 %all-reduce.5.cloned.1.call-start = ((), (), s32[]{:S(2)}) async-start(), calls=%async_computation.3 | async-start | bytes 262144 | tf_op jit(solution)/shard_map/while/body/eval_jaxpr/psum | solution.py:28
  3026.6 78.8 %all-reduce.5.cloned.1.call-start = ((), (), s32[]{:S(2)}) async-start(), calls=%async_computation.3 | async-start | bytes 262144 | tf_op jit(solution)/shard_map/while/body/eval_jaxpr/psum | solution.py:28
  3473.5 78.8 %all-reduce.5.cloned.1.call-start = ((), (), s32[]{:S(2)}) async-start(), calls=%async_computation.3 | async-start | bytes 262144 | tf_op jit(solution)/shard_map/while/body/eval_jaxpr/psum | solution.py:28
  3563.1 78.8 %all-reduce.5.cloned.1.call-start = ((), (), s32[]{:S(2)}) async-start(), calls=%async_computation.3 | async-start | bytes 262144 | tf_op jit(solution)/shard_map/while/body/eval_jaxpr/psum | solution.py:28
  4010.0 78.8 %all-reduce.5.cloned.1.call-start = ((), (), s32[]{:S(2)}) async-start(), calls=%async_computation.3 | async-start | bytes 262144 | tf_op jit(solution)/shard_map/while/body/eval_jaxpr/psum | solution.py:28
  4188.9 78.8 %all-reduce.5.cloned.1.call-start = ((), (), s32[]{:S(2)}) async-start(), calls=%async_computation.3 | async-start | bytes 262144 | tf_op jit(solution)/shard_map/while/body/eval_jaxpr/psum | solution.py:28
  4278.6 78.8 %all-reduce.5.cloned.1.call-start = ((), (), s32[]{:S(2)}) async-start(), calls=%async_computation.3 | async-start | bytes 262144 | tf_op jit(solution)/shard_map/while/body/eval_jaxpr/psum | solution.py:28
  4546.9 78.8 %all-reduce.5.cloned.1.call-start = ((), (), s32[]{:S(2)}) async-start(), calls=%async_computation.3 | async-start | bytes 262144 | tf_op jit(solution)/shard_map/while/body/eval_jaxpr/psum | solution.py:28
  4725.8 78.8 %all-reduce.5.cloned.1.call-start = ((), (), s32[]{:S(2)}) async-start(), calls=%async_computation.3 | async-start | bytes 262144 | tf_op jit(solution)/shard_map/while/body/eval_jaxpr/psum | solution.py:28
  4815.4 78.8 %all-reduce.5.cloned.1.call-start = ((), (), s32[]{:S(2)}) async-start(), calls=%async_computation.3 | async-start | bytes 262144 | tf_op jit(solution)/shard_map/while/body/eval_jaxpr/psum | solution.py:28
  4905.0 78.8 %all-reduce.5.cloned.1.call-start = ((), (), s32[]{:S(2)}) async-start(), calls=%async_computation.3 | async-start | bytes 262144 | tf_op jit(solution)/shard_map/while/body/eval_jaxpr/psum | solution.py:28
  4994.7 78.8 %all-reduce.5.cloned.1.call-start = ((), (), s32[]{:S(2)}) async-start(), calls=%async_computation.3 | async-start | bytes 262144 | tf_op jit(solution)/shard_map/while/body/eval_jaxpr/psum | solution.py:28
  5084.3 78.8 %all-reduce.5.cloned.1.call-start = ((), (), s32[]{:S(2)}) async-start(), calls=%async_computation.3 | async-start | bytes 262144 | tf_op jit(solution)/shard_map/while/body/eval_jaxpr/psum | solution.py:28
  5173.9 78.8 %all-reduce.5.cloned.1.call-start = ((), (), s32[]{:S(2)}) async-start(), calls=%async_computation.3 | async-start | bytes 262144 | tf_op jit(solution)/shard_map/while/body/eval_jaxpr/psum | solution.py:28
  5352.9 78.8 %all-reduce.5.cloned.1.call-start = ((), (), s32[]{:S(2)}) async-start(), calls=%async_computation.3 | async-start | bytes 262144 | tf_op jit(solution)/shard_map/while/body/eval_jaxpr/psum | solution.py:28
  5442.5 78.8 %all-reduce.5.cloned.1.call-start = ((), (), s32[]{:S(2)}) async-start(), calls=%async_computation.3 | async-start | bytes 262144 | tf_op jit(solution)/shard_map/while/body/eval_jaxpr/psum | solution.py:28
  5621.4 78.8 %all-reduce.5.cloned.1.call-start = ((), (), s32[]{:S(2)}) async-start(), calls=%async_computation.3 | async-start | bytes 262144 | tf_op jit(solution)/shard_map/while/body/eval_jaxpr/psum | solution.py:28
  5711.1 78.8 %all-reduce.5.cloned.1.call-start = ((), (), s32[]{:S(2)}) async-start(), calls=%async_computation.3 | async-start | bytes 262144 | tf_op jit(solution)/shard_map/while/body/eval_jaxpr/psum | solution.py:28
  (162 other events, 7937.0 us)
Sparse Core Ops, SparseCore 0:
  74.7 52.5 all-reduce.2
  343.3 52.2 all-reduce.2
  521.9 52.2 all-reduce.2
  611.3 52.2 all-reduce.2
  789.9 52.2 all-reduce.2
  879.2 52.2 all-reduce.2
  968.8 52.2 all-reduce.2
  1147.5 52.2 all-reduce.2
  1237.1 52.2 all-reduce.2
  1326.5 52.2 all-reduce.2
  1505.7 52.2 all-reduce.2
  1595.0 52.2 all-reduce.2
  1684.7 52.2 all-reduce.2
  1774.3 52.2 all-reduce.2
  2221.8 52.2 all-reduce.2
  2580.0 52.2 all-reduce.2
  3295.4 52.2 all-reduce.2
  3384.7 52.2 all-reduce.2
  3831.9 52.2 all-reduce.2
  3921.3 52.2 all-reduce.2
  4010.9 52.2 all-reduce.2
  4189.8 52.2 all-reduce.2
  4279.5 52.2 all-reduce.2
  4368.8 52.2 all-reduce.2
  4458.1 52.2 all-reduce.2
  4905.9 52.2 all-reduce.2
  5085.2 52.2 all-reduce.2
  5174.8 52.2 all-reduce.2
  5264.2 52.2 all-reduce.2
  5443.4 52.2 all-reduce.2
  5532.7 52.2 all-reduce.2
  5622.4 52.2 all-reduce.2
  (97 shorter events, 2868.0 us)
where the time goes:
time: 5810 us; the launch traced here: 5800 us
  waiting for transfers between devices  4620 us (80%)
  matrix products  950 us (16%)
  other arithmetic  198 us (3%)
    psum x64, waiting for transfers between devices, panel_step(): v_pan = lax.psum(jnp.where(my_col == owner_col, v_blk, 0.0), 'col')  3390 us
    psum x64, waiting for transfers between devices, panel_step(): w_full = lax.psum(w_part, 'row')  1180 us
    dot_general x64, matrix products, panel_step(): jnp.einsum('nb,nk->bk', v_pan, x_cur, preferred_element_type=jnp.float32,...  456 us
    dot_general x64, matrix products, panel_step(): jnp.dot(v_pan, y_blk, preferred_element_type=jnp.float32, precision=FULL_...  417 us
    select_n x64, other arithmetic, panel_step(): v_pan = lax.psum(jnp.where(my_col == owner_col, v_blk, 0.0), 'col')  198 us
  transfers between devices with their start and end apart: 130, of which 129 were waited for; matrix products, arithmetic and copies ran while one was open for 0% of the time, Pallas kernels for 0%

commit v1 on v0

v1 whole, which is shorter than its diff:
```python
import functools

import jax
import jax.numpy as jnp
from jax import lax
from jax.experimental import pallas as pl
from jax.experimental.pallas import tpu as pltpu
from jax.sharding import PartitionSpec as P

F32 = jnp.float32
BF16 = jnp.bfloat16
MESH_ID = pl.DeviceIdType.MESH

NB = 128
PW = 2 * NB
CH = 4 * NB
RING = 4


def split3(x):
    hi = x.astype(BF16)
    rest = x - hi.astype(F32)
    mid = rest.astype(BF16)
    low = (rest - mid.astype(F32)).astype(BF16)
    return hi, mid, low


def mm(a, b):
    return lax.dot_general(a, b, (((1,), (0,)), ((), ())), preferred_element_type=F32)


def mm_nt(a, b):
    return lax.dot_general(a, b, (((1,), (1,)), ((), ())), preferred_element_type=F32)


def stacked(dot, a3, b_hi, b_mid, b_low):
    m = a3.shape[0] // 3
    r = dot(a3, b_hi)
    s = r[0:m] + r[m : 2 * m] + r[2 * m : 3 * m]
    r = dot(a3[0 : 2 * m], b_mid)
    s = s + r[0:m] + r[m : 2 * m]
    return s + dot(a3[0:m], b_low)


def full_dot(dot, a, b):
    ah, am, al = split3(a)
    bh, bm, bl = split3(b)
    return stacked(dot, jnp.concatenate([ah, am, al], axis=0), bh, bm, bl)


def body(nsb, v_ref, t_ref, z_ref, out_ref, vb, *s):
    (zl, xt, xp, vf, vn, tb, tp, ws, wr, gs, gr, yp,
     z_loc, z_snd, z_rcv, i_rcv, d_rcv, w_snd, w_rcv, g_snd, g_rcv, ld, o_sem, i_snd, d_snd) = s
    rows = nsb * CH
    npair = nsb * RING
    r = lax.axis_index("row")
    col = lax.axis_index("col")
    q = col % 2
    k = col // 2
    ky, kx = k // 2, k % 2
    rho = 2 * ky + (kx + ky) % 2

    def at_ring(i):
        i = i % RING
        y = i // 2
        x = (i % 2 + y) % 2
        return (r, (y * 2 + x) * 2 + q)

    partner = (r, k * 2 + 1 - q)
    across = (1 - r, col)

    def pair_of(t):
        return npair - 1 - t

    def sb_of(t):
        return pair_of(t) // RING

    def owner_dist(t):
        kk = pair_of(t) % RING
        y = kk // 2
        ro = 2 * y + (kk % 2 + y) % 2
        return (rho - ro + RING) % RING

    def by_chunk(t, c, fn):
        l = sb_of(t)
        kk = pair_of(t) % RING

        @pl.when(c > l)
        def _():
            fn(pl.multiple_of(c * CH, CH), CH)

        for j in range(RING):

            @pl.when((c == l) & (kk == j))
            def _(j=j):
                fn(pl.multiple_of(c * CH + j * NB, NB), CH - j * NB)

    def own_rows(t, r0, n):
        return v_ref.at[pl.ds(r0, n), pl.ds(pl.multiple_of(sb_of(t) * NB, NB), NB)]

    def copy(src, dst, ssem, rsem, dev):
        return pltpu.make_async_remote_copy(src, dst, ssem, rsem, device_id=dev, device_id_type=MESH_ID)

    def ici(t, c, r0, n, half, own):
        src = own_rows(t, r0, n) if own else vb.at[q, pair_of(t), pl.ds(r0, n), :]
        return copy(src, vb.at[q, pair_of(t), pl.ds(r0, n), :], i_snd.at[t % 8, c], i_rcv.at[t, c],
                    at_ring(rho + 1 - 2 * half + RING))

    def d2d(t, c, r0, n, own):
        src = own_rows(t, r0, n) if own else vb.at[q, pair_of(t), pl.ds(r0, n), :]
        return copy(src, vb.at[q, pair_of(t), pl.ds(r0, n), :], d_snd.at[t % 8, c], d_rcv.at[t, c], partner)

    def ici_t(t, own):
        src = t_ref.at[sb_of(t)] if own else tb.at[q, pair_of(t)]
        return copy(src, tb.at[q, pair_of(t)], i_snd.at[t % 8, nsb], i_rcv.at[t, nsb], at_ring(rho - 1 + RING))

    def d2d_t(t, own):
        src = t_ref.at[sb_of(t)] if own else tb.at[q, pair_of(t)]
        return copy(src, tb.at[q, pair_of(t)], d_snd.at[t % 8, nsb], d_rcv.at[t, nsb], partner)

    def wait_sent(t, c, ring):
        def fn(r0, n):
            if ring:
                ici(t, c, r0, n, 0, False).wait_send()
            d2d(t, c, r0, n, False).wait_send()

        by_chunk(t, c, fn)

    def wait_sent_t(t, ring):
        if ring:
            ici_t(t, False).wait_send()
        d2d_t(t, False).wait_send()

    def send_own(t):
        l = sb_of(t)

        def one(c, _):
            half = (c - l) % 2

            @pl.when((t >= 8) & (c >= sb_of(t - 8)))
            def _():
                wait_sent(t - 8, c, True)

            def fn(r0, n):
                ici(t, c, r0, n, half, True).start()
                d2d(t, c, r0, n, True).start()

            by_chunk(t, c, fn)
            return 0

        lax.fori_loop(l, nsb, one, 0)

        @pl.when(t >= 8)
        def _():
            wait_sent_t(t - 8, True)

        ici_t(t, True).start()
        d2d_t(t, True).start()

    def pass_on(t, half, hop):
        l = sb_of(t)
        forward = hop < RING - 1

        def one(i, _):
            c = l + half + 2 * i

            def got(r0, n):
                ici(t, c, r0, n, half, False).wait_recv()

            by_chunk(t, c, got)

            @pl.when((t >= 8) & (c >= sb_of(t - 8)))
            def _():
                @pl.when(forward)
                def _():
                    wait_sent(t - 8, c, True)

                @pl.when(jnp.logical_not(forward))
                def _():
                    wait_sent(t - 8, c, False)

            def fn(r0, n):
                d2d(t, c, r0, n, False).start()

                @pl.when(forward)
                def _():
                    ici(t, c, r0, n, half, False).start()

            by_chunk(t, c, fn)
            return 0

        lax.fori_loop(0, (nsb - l - half + 1) // 2, one, 0)

        @pl.when(half == 1)
        def _():
            ici_t(t, False).wait_recv()

            @pl.when(t >= 8)
            def _():
                @pl.when(forward)
                def _():
                    wait_sent_t(t - 8, True)

                @pl.when(jnp.logical_not(forward))
                def _():
                    wait_sent_t(t - 8, False)

            d2d_t(t, False).start()

            @pl.when(forward)
            def _():
                ici_t(t, False).start()

    def service(slot):
        def hops(j, _):
            hop = RING - 1 - j // 2
            half = j % 2
            t = slot + 6 - 2 * hop
            d = owner_dist(t)
            arrives = jnp.where(half == 0, d, RING - d)

            @pl.when((t >= 0) & (t < npair) & (arrives == hop))
            def _():
                pass_on(t, half, hop)

            return 0

        lax.fori_loop(0, 6, hops, 0)
        t = slot + 6

        @pl.when((t >= 0) & (t < npair) & (owner_dist(t) == 0))
        def _():
            send_own(t)

    def lead(i):
        return jnp.clip(jnp.minimum(i + 1, (24 - i) // 4), 0, 2)

    def last_slot(i):
        return jnp.minimum(i + 1 + lead(i), npair - 1)

    def z_copies(c):
        r0 = pl.multiple_of(c * CH, CH)
        mine = pl.multiple_of(r * rows + c * CH, CH)
        theirs = pl.multiple_of((1 - r) * rows + c * CH, CH)
        loc = pltpu.make_async_copy(z_ref.at[pl.ds(mine, CH), :], zl.at[r, pl.ds(r0, CH), :], z_loc.at[c])
        rem = copy(z_ref.at[pl.ds(theirs, CH), :], zl.at[r, pl.ds(r0, CH), :], z_snd.at[c], z_rcv.at[c], across)
        return loc, rem

    def start_z(c):
        loc, rem = z_copies(c)
        loc.start()
        rem.start()

    def admit(c):
        loc, rem = z_copies(c)
        loc.wait()
        rem.wait()
        r0 = pl.multiple_of(c * CH, CH)

        def one(g, _):
            x = zl[g, pl.ds(r0, CH), :].T
            xt[g, :, pl.ds(r0, CH)] = x
            h, m, lo = split3(x)
            xp[g, 0:NB, pl.ds(r0, CH)] = h
            xp[g, NB : 2 * NB, pl.ds(r0, CH)] = m
            xp[g, 2 * NB : 3 * NB, pl.ds(r0, CH)] = lo
            return 0

        lax.fori_loop(0, 2, one, 0)

    def load(t, c, side, r0, n):
        src = vb.at[side, pair_of(t), pl.ds(r0, n), :]
        return pltpu.make_async_copy(
            src, vf.at[pl.ds(r0, n), pl.ds(pl.multiple_of(side * NB, NB), NB)], ld.at[side, c])

    def load_own(t, c, r0, n):
        return pltpu.make_async_copy(
            own_rows(t, r0, n), vf.at[pl.ds(r0, n), pl.ds(pl.multiple_of(q * NB, NB), NB)], ld.at[q, c])

    def t_own(t):
        return pltpu.make_async_copy(t_ref.at[sb_of(t)], tb.at[q, pair_of(t)], ld.at[q, nsb])

    def start_loads(t):
        l = sb_of(t)
        mine = owner_dist(t) == 0

        def one(c, _):
            def fn(r0, n):
                @pl.when(mine)
                def _():
                    load_own(t, c, r0, n).start()

                @pl.when(jnp.logical_not(mine))
                def _():
                    load(t, c, q, r0, n).start()

                d2d(t, c, r0, n, False).wait_recv()
                load(t, c, 1 - q, r0, n).start()

            by_chunk(t, c, fn)
            return 0

        lax.fori_loop(l, nsb, one, 0)

        @pl.when(mine)
        def _():
            t_own(t).start()

        d2d_t(t, False).wait_recv()

    def prep(t):
        l = sb_of(t)
        first = pair_of(t) * NB
        slot = t % 2

        def one(c, _):
            def fn(r0, n):
                load(t, c, 0, r0, n).wait()
                load(t, c, 1, r0, n).wait()

            by_chunk(t, c, fn)

            def sub(j, _):
                r0 = pl.multiple_of(c * CH + j * NB, NB)
                x = vf[pl.ds(r0, NB), :]
                x = jnp.where(lax.broadcasted_iota(jnp.int32, (NB, PW), 0) + r0 >= first, x, 0.0)
                h, m, lo = split3(x)
                vn[slot, pl.ds(r0, NB), 0:PW] = h
                vn[slot, pl.ds(r0, NB), PW : 2 * PW] = m
                vn[slot, pl.ds(r0, NB), 2 * PW : 3 * PW] = lo
                return 0

            lax.fori_loop(0, CH // NB, sub, 0)
            return 0

        lax.fori_loop(l, nsb, one, 0)

        @pl.when(owner_dist(t) == 0)
        def _():
            t_own(t).wait()

    def gram_copy(t):
        return copy(gs.at[t % 2], gr.at[t % 2], g_snd.at[t % 2], g_rcv.at[t % 2], across)

    def gram(t):
        slot = t % 2

        @pl.when(t >= 2)
        def _():
            gram_copy(t - 2).wait_send()

        gs[slot] = jnp.zeros((NB, NB), F32)

        def one(c, _):
            r0 = pl.multiple_of(c * CH, CH)
            a3 = jnp.concatenate(
                [vn[slot, pl.ds(r0, CH), i * PW : i * PW + NB].T for i in range(3)], axis=0)
            b = [vn[slot, pl.ds(r0, CH), i * PW + NB : (i + 1) * PW] for i in range(3)]
            gs[slot] += stacked(mm, a3, *b)
            return 0

        lax.fori_loop(sb_of(t), nsb, one, 0)
        gram_copy(t).start()

    def block_factor(t):
        slot = t % 2
        gram_copy(t).wait_recv()
        g = gs[slot] + gr[slot]
        ta = tb[0, pair_of(t)]
        tbb = tb[1, pair_of(t)]
        upper = -full_dot(mm, ta, full_dot(mm, g, tbb))
        for i, piece in enumerate(split3(ta)):
            tp[0:NB, i * PW : i * PW + NB] = piece
        for i, piece in enumerate(split3(upper)):
            tp[0:NB, i * PW + NB : (i + 1) * PW] = piece
        for i, piece in enumerate(split3(tbb)):
            tp[NB:PW, i * PW : i * PW + NB] = jnp.zeros((NB, NB), BF16)
            tp[NB:PW, i * PW + NB : (i + 1) * PW] = piece

    def w_copy(t, g):
        return copy(ws.at[t % 2, g], wr.at[t % 2, g], w_snd.at[t % 2, g], w_rcv.at[t % 2, g], across)

    def coefficients(t, g):
        w_copy(t, g).wait_recv()
        w = ws[t % 2, g] + wr[t % 2, g]
        y = stacked(mm_nt, jnp.concatenate(split3(w), axis=0),
                    tp[:, 0:PW], tp[:, PW : 2 * PW], tp[:, 2 * PW : 3 * PW])
        h, m, lo = split3(y)
        yp[0:NB] = h
        yp[NB : 2 * NB] = m
        yp[2 * NB : 3 * NB] = lo

    def update(t, g, c):
        r0 = pl.multiple_of(c * CH, CH)
        slot = t % 2
        b = [vn[slot, pl.ds(r0, CH), i * PW : (i + 1) * PW] for i in range(3)]
        x = xt[g, :, pl.ds(r0, CH)] - stacked(mm_nt, yp[...], *b)
        xt[g, :, pl.ds(r0, CH)] = x
        h, m, lo = split3(x)
        xp[g, 0:NB, pl.ds(r0, CH)] = h
        xp[g, NB : 2 * NB, pl.ds(r0, CH)] = m
        xp[g, 2 * NB : 3 * NB, pl.ds(r0, CH)] = lo

    def product(t, g, c):
        r0 = pl.multiple_of(c * CH, CH)
        slot = t % 2
        b = [vn[slot, pl.ds(r0, CH), i * PW : (i + 1) * PW] for i in range(3)]
        ws[slot, g] += stacked(mm, xp[g, :, pl.ds(r0, CH)], *b)

    def both(i, g):
        c0 = sb_of(i)
        c1 = sb_of(i + 1)
        n = i + 1
        update(i, g, c0)

        @pl.when(c1 < c0)
        def _():
            product(n, g, c1)

        def one(c, _):
            product(n, g, c - 1)
            update(i, g, c)
            return 0

        lax.fori_loop(c0 + 1, nsb, one, 0)
        product(n, g, nsb - 1)

    def step(i, _):
        n = i + 1

        @pl.when(i >= 0)
        def _():
            @pl.when((i % RING == 0) & (i // RING + 2 < nsb))
            def _():
                start_z(nsb - 1 - (i // RING + 2))

        @pl.when(n < npair)
        def _():
            first = jnp.where(i < 0, -6, last_slot(i - 1) + 1)
            lax.fori_loop(first, last_slot(i) + 1, lambda slot, _: (service(slot), 0)[1], 0)
            start_loads(n)

        @pl.when(i >= 0)
        def _():
            block_factor(i)

        @pl.when(n < npair)
        def _():
            prep(n)
            gram(n)

            @pl.when(n % RING == 0)
            def _():
                admit(sb_of(n))

        def group(g, _):
            @pl.when(i >= 0)
            def _():
                coefficients(i, g)

            @pl.when(n < npair)
            def _():
                @pl.when(n >= 2)
                def _():
                    w_copy(n - 2, g).wait_send()

                ws[n % 2, g] = jnp.zeros((NB, PW), F32)

            @pl.when(i < 0)
            def _():
                product(n, g, nsb - 1)

            @pl.when((i >= 0) & (n < npair))
            def _():
                both(i, g)

            @pl.when(n < npair)
            def _():
                w_copy(n, g).start()

            @pl.when(n == npair)
            def _():
                def one(c, _):
                    update(i, g, c)
                    r0 = pl.multiple_of(c * CH, CH)
                    zl[g, pl.ds(r0, CH), :] = xt[g, :, pl.ds(r0, CH)].T
                    out_copy(g, c).start()
                    return 0

                lax.fori_loop(0, nsb, one, 0)

            return 0

        lax.fori_loop(0, 2, group, 0)
        return 0

    def out_copy(g, c):
        r0 = pl.multiple_of(c * CH, CH)
        return pltpu.make_async_copy(
            zl.at[g, pl.ds(r0, CH), :],
            out_ref.at[pl.ds(r0, CH), pl.ds(pl.multiple_of(g * NB, NB), NB)], o_sem.at[g, c])

    barrier = pltpu.get_barrier_semaphore()
    for dev in (at_ring(rho + 1), at_ring(rho + RING - 1), partner, across):
        pl.semaphore_signal(barrier, inc=1, device_id=dev, device_id_type=MESH_ID)
    pl.semaphore_wait(barrier, 4)

    start_z(nsb - 1)
    if nsb > 1:
        start_z(nsb - 2)
    lax.fori_loop(-1, npair, step, 0)

    for t in (npair - 2, npair - 1):
        gram_copy(t).wait_send()
        for g in range(2):
            w_copy(t, g).wait_send()

    def drain(t, _):
        d = owner_dist(t)

        def one(c, _):
            half = (c - sb_of(t)) % 2
            hop = jnp.where(half == 0, d, (RING - d) % RING)

            @pl.when(hop < RING - 1)
            def _():
                wait_sent(t, c, True)

            @pl.when(hop == RING - 1)
            def _():
                wait_sent(t, c, False)

            return 0

        lax.fori_loop(sb_of(t), nsb, one, 0)

        @pl.when(d != 1)
        def _():
            wait_sent_t(t, True)

        @pl.when(d == 1)
        def _():
            wait_sent_t(t, False)

        return 0

    lax.fori_loop(max(0, npair - 8), npair, drain, 0)

    def out_done(c, _):
        for g in range(2):
            out_copy(g, c).wait()
        return 0

    lax.fori_loop(0, nsb, out_done, 0)


def solution(mesh):
    def local(v, t, z):
        rows, cols = v.shape
        nsb = cols // NB
        npair = nsb * RING
        dma = pltpu.SemaphoreType.DMA
        hbm = pl.BlockSpec(memory_space=pltpu.MemorySpace.HBM)
        out, _ = pl.pallas_call(
            functools.partial(body, nsb),
            out_shape=(
                jax.ShapeDtypeStruct((rows, PW), F32),
                jax.ShapeDtypeStruct((2, npair, rows, NB), F32),
            ),
            in_specs=[hbm] * 3,
            out_specs=(hbm, hbm),
            scratch_shapes=[
                pltpu.VMEM((2, rows, NB), F32),
                pltpu.VMEM((2, NB, rows), F32),
                pltpu.VMEM((2, 3 * NB, rows), BF16),
                pltpu.VMEM((rows, PW), F32),
                pltpu.VMEM((2, rows, 3 * PW), BF16),
                pltpu.VMEM((2, npair, NB, NB), F32),
                pltpu.VMEM((PW, 3 * PW), BF16),
                pltpu.VMEM((2, 2, NB, PW), F32),
                pltpu.VMEM((2, 2, NB, PW), F32),
                pltpu.VMEM((2, NB, NB), F32),
                pltpu.VMEM((2, NB, NB), F32),
                pltpu.VMEM((3 * NB, PW), BF16),
                dma((nsb,)),
                dma((nsb,)),
                dma((nsb,)),
                dma((npair, nsb + 1)),
                dma((npair, nsb + 1)),
                dma((2, 2)),
                dma((2, 2)),
                dma((2,)),
                dma((2,)),
                dma((2, nsb + 1)),
                dma((2, nsb)),
                dma((8, nsb + 1)),
                dma((8, nsb + 1)),
            ],
            compiler_params=pltpu.CompilerParams(
                collective_id=0, has_side_effects=True, vmem_limit_bytes=60 * 2**20),
            name="backtransform",
        )(v, t, z)
        return out

    return jax.shard_map(local, mesh=mesh,
                         in_specs=(P("row", "col"), P("col", None, None), P(None, ("col", "row"))),
                         out_specs=P("row", "col"), check_vma=False)
```

time: 5810 us -> 496 us (0.09)
  waiting for transfers between devices: 4620 us -> 0 us
  matrix products: 950 us -> 0 us
  Pallas kernels: 0 us -> 491 us
  other arithmetic: 198 us -> 0 us
    psum x128 -> x0, waiting for transfers between devices: 4570 us -> none  [the longest x64 3390 us: panel_step(): v_pan = lax.psum(jnp.where(my_col == owner_col, v_blk, 0.0), 'col')]
    dot_general x192 -> x0, matrix products: 950 us -> none  [the longest x64 456 us: panel_step(): jnp.einsum('nb,nk->bk', v_pan, x_cur, preferred_element_type=jnp.float32,...]
    pallas_call x0 -> x1, Pallas kernels: none -> 491 us  [local(): pl.pallas_call(functools.partial(body, nsb), out_shape=(jax.ShapeDtypeStr...]
    select_n x64 -> x0, other arithmetic: 198 us -> none  [panel_step(): v_pan = lax.psum(jnp.where(my_col == owner_col, v_blk, 0.0), 'col')]
  transfers between devices with their start and end apart: 130 -> 0, of which waited for: 129 -> 0; matrix products, arithmetic and copies ran while one was open for 0% -> 0% of each run, Pallas kernels for 0% -> 0%
where the time goes in v1:
time: 496 us
  Pallas kernels  491 us (99%)
    pallas_call x1, Pallas kernels, local(): pl.pallas_call(functools.partial(body, nsb), out_shape=(jax.ShapeDtypeStr...  491 us

profile of v1, /device:TPU:5, one launch (start us, length us, event | category | flops | bytes accessed | tf_op | source)
XLA Modules:
  0.0 495.6 jit_solution(11644913097192581008)
XLA Ops:
  0.0 491.1 %backtransform.1 = (f32[4096,256]{1,0:T(8,128)}, f32[2,32,4096,128]{3,2,1,0:T(8,128)}) custom-call(f32[4096,1024]{1,0:T(8,128)} %v_ref.1, f32[8,128,128]{2,1,0:T(8,128)} %t_ref.1, f32[8192,128]{1,0:T(8,128)} %z_ref.1), custom_call_target="tpu_custom_call" | custom-call | tf_op jit(solution)/shard_map/backtransform/pallas_call | solution.py:564
  491.1 4.5 copy.5
